TPU v7x, 32 devices: a whole 2x2x4 slice. The times are simulated.
32 devices in a mesh: gx: 4 (over y, x), gy: 8 (over z, core).
Axes of the slice: x: 2, y: 2, z: 4, core: 2. Of those that a mesh axis runs over, the one named last changes fastest.
Arguments:
- voltages: bfloat16 [2, 2048, 122880], P(None, ('gx', 'gy')), may hold values from -6 to 6
- gains: float32 [2, 2048, 8192], P(None, ('gx', 'gy')), may hold values from -6 to 6
- delays: float32 [64, 2048], replicated, may hold values from -32 to 32
- channel_order: int32 [4, 8], replicated, may hold values from 0 to 7, each once within a row
- beam_table: int32 [64], replicated, may hold values from 0 to 63, each once
Outputs:
- beam_power: float32 [64, 4, 8192], P('gy', None, 'gx')
Inputs may be any that keep to these rules, and one draw needn't show every extreme that they name: Each row names every index of gy once; channel block a * 8 + channel_order[a, b] of 256 channels belongs to the device at gx = a, gy = b. Names every beam once; the beams beam_table[g * 64 / 8] onward, 64 / 8 of them, belong to gy index g.
All inputs are finite; a program needn't handle non-finite values.
Results may differ from a plain program's by a relative error of at most 0.009.
Values may be sent and summed in bfloat16 or wider, within the bound.
No kernel may reach another device: no remote copies, remote signals or barrier semaphores. Data moves between devices by JAX's collectives and lax.ppermute only.
A program may use at most 192 MiB of HBM per device.

v0:
```python
import math

import jax
import jax.numpy as jnp
from jax import lax
from jax.sharding import PartitionSpec as P

NIN = 2048
NCH = 8192
NBEAM = 64
TAPS = 8
INTEG = 2
NSPEC = 8
TIMES = 4


def coefficients():
    total = TAPS * NCH
    index = jnp.arange(total, dtype=jnp.float32)
    offset = (index - total / 2) / NCH
    window = 0.5 - 0.5 * jnp.cos(2.0 * math.pi * index / total)
    raw = jnp.sinc(offset) * window
    raw = raw / jnp.sqrt(jnp.sum(raw * raw) / NCH)
    return raw.reshape(TAPS, NCH)


def transform(filtered):
    first_len = 64
    second_len = NCH // first_len
    first_ids = jnp.arange(first_len, dtype=jnp.int32)
    second_ids = jnp.arange(second_len, dtype=jnp.int32)
    small_angle = (
        2.0
        * math.pi
        / first_len
        * (first_ids[:, None] * first_ids[None, :] % first_len).astype(jnp.float32)
    )
    small_cos = jnp.cos(small_angle)
    small_sin = -jnp.sin(small_angle)
    small_stack = jnp.concatenate(
        [
            jnp.concatenate([small_cos, -small_sin], axis=1),
            jnp.concatenate([small_sin, small_cos], axis=1),
        ],
        axis=0,
    ).astype(jnp.bfloat16)
    twist_angle = (
        2.0 * math.pi / NCH * (first_ids[:, None] * second_ids[None, :]).astype(jnp.float32)
    )
    twist_cos = jnp.cos(twist_angle)
    twist_sin = -jnp.sin(twist_angle)
    large_angle = (
        2.0
        * math.pi
        / second_len
        * (second_ids[:, None] * second_ids[None, :] % second_len).astype(jnp.float32)
    )
    large_cos = jnp.cos(large_angle)
    large_sin = -jnp.sin(large_angle)
    large_stack = jnp.concatenate(
        [
            jnp.concatenate([large_cos, large_sin], axis=1),
            jnp.concatenate([-large_sin, large_cos], axis=1),
        ],
        axis=0,
    ).astype(jnp.bfloat16)
    inputs_here = filtered.shape[1]
    spectra_here = filtered.shape[2]
    stacked = jnp.transpose(
        filtered.reshape(2, inputs_here, spectra_here, first_len, second_len), (1, 2, 0, 3, 4)
    ).reshape(inputs_here, spectra_here, 2 * first_len, second_len)
    inner = jnp.einsum("km,ismq->iskq", small_stack, stacked, preferred_element_type=jnp.float32)
    inner_real = inner[:, :, :first_len]
    inner_imag = inner[:, :, first_len:]
    turned_real = inner_real * twist_cos - inner_imag * twist_sin
    turned_imag = inner_real * twist_sin + inner_imag * twist_cos
    turned = jnp.concatenate([turned_real, turned_imag], axis=3).astype(jnp.bfloat16)
    outer = jnp.einsum("iskq,qn->isnk", turned, large_stack, preferred_element_type=jnp.float32)
    scale = NCH ** (-0.5)
    outer_real = outer[:, :, :second_len].reshape(inputs_here, spectra_here, NCH) * scale
    outer_imag = outer[:, :, second_len:].reshape(inputs_here, spectra_here, NCH) * scale
    return (outer_real, outer_imag)


def body(voltages, gains, delays, channel_order, beam_table):
    across = lax.axis_size("gx")
    along = lax.axis_size("gy")
    devices = across * along
    inputs_here = voltages.shape[1]
    width = NCH // devices
    beams_here = NBEAM // along
    frames = voltages.reshape(2, inputs_here, NSPEC + TAPS - 1, NCH)
    taps_table = coefficients()
    filtered = taps_table[0] * frames[:, :, 0:NSPEC].astype(jnp.float32)
    for tap_index in range(1, TAPS):
        filtered = filtered + taps_table[tap_index] * frames[
            :, :, tap_index : tap_index + NSPEC
        ].astype(jnp.float32)
    spec_real, spec_imag = transform(filtered.astype(jnp.bfloat16))
    gain_real = gains[0][:, None, :]
    gain_imag = gains[1][:, None, :]
    calibrated = jnp.stack(
        [
            gain_real * spec_real - gain_imag * spec_imag,
            gain_real * spec_imag + gain_imag * spec_real,
        ]
    ).astype(jnp.bfloat16)
    order = (jnp.arange(across, dtype=jnp.int32)[:, None] * along + channel_order).reshape(-1)
    blocks = jnp.take(calibrated.reshape(2, inputs_here, NSPEC, devices, width), order, axis=3)
    column = lax.axis_index("gx")
    member = lax.axis_index("gy")
    owned = column * along + channel_order[column, member]
    channel = (owned * width + jnp.arange(width, dtype=jnp.int32)).astype(jnp.float32)
    offsets = jnp.take(delays, beam_table, axis=0)
    phase = channel[:, None, None] * offsets[None] * (-2.0 * math.pi / NCH)
    scale = NIN ** (-0.5)
    weight_real = (jnp.cos(phase) * scale).astype(jnp.bfloat16)
    weight_imag = (jnp.sin(phase) * scale).astype(jnp.bfloat16)
    piece = lax.all_to_all(blocks, ("gx", "gy"), split_axis=3, concat_axis=1, tiled=True)[
        :, :, :, 0, :
    ]
    first = jnp.einsum("cbi,pisc->cbps", weight_real, piece, preferred_element_type=jnp.float32)
    second = jnp.einsum("cbi,pisc->cbps", weight_imag, piece, preferred_element_type=jnp.float32)
    beam_real = (first[:, :, 0] - second[:, :, 1]).astype(jnp.bfloat16)
    beam_imag = (first[:, :, 1] + second[:, :, 0]).astype(jnp.bfloat16)
    voltage_beams = jnp.stack([beam_real, beam_imag], axis=2)
    local_real = voltage_beams[:, :, 0].astype(jnp.float32)
    local_imag = voltage_beams[:, :, 1].astype(jnp.float32)
    local_power = (
        (local_real * local_real + local_imag * local_imag)
        .reshape(width, NBEAM, TIMES, INTEG)
        .sum(axis=3)
    )
    power = lax.all_to_all(
        local_power[None].astype(jnp.bfloat16), "gy", split_axis=2, concat_axis=0, tiled=True
    ).astype(jnp.float32)
    return jnp.transpose(power, (2, 3, 0, 1)).reshape(beams_here, TIMES, along * width)


def solution(mesh):
    return jax.shard_map(
        body,
        mesh=mesh,
        in_specs=(P(None, ("gx", "gy"), None), P(None, ("gx", "gy"), None), P(), P(), P()),
        out_specs=P("gy", None, "gx"),
        check_vma=False,
    )
```

profile of v0, /device:TPU:0, one launch (start us, length us, event | category | flops | bytes accessed | tf_op | source)
XLA Modules:
  0.0 1713.4 jit_solution(11769270986124165315)
XLA Ops:
  0.0 1.9 multiply_reduce_fusion
  6.9 36.2 %reshape.232 = bf16[2,64,15,8192]{3,2,1,0:T(8,128)(2,1)} reshape(bf16[2,64,122880]{2,1,0:T(8,128)(2,1)} %param.5) | data formatting | bytes 62914560 | tf_op jit(solution)/shard_map/reshape | solution.py:92
  43.1 85.1 %fusion.10 = bf16[64,8,2,64,128]{4,1,3,0,2:T(8,128)(2,1)} fusion(bf16[2,64,15,8192]{3,2,1,0:T(8,128)(2,1)} %reshape.232, f32[8192]{0:T(1024)S(1)} %get-tuple-element.14, f32[8192]{0:T(1024)S(1)} %get-tuple-element.15, f32[8192]{0:T(1024)S(1)} %get-tuple-element.16, f32[8192]{0:T(1024)S(1)} %get-tuple-element.17, f32[8192]{0:T(1024)S(1)} %get-tuple-element.18, ...), kind=kLoop, calls=%fused_computation.20 | loop fusion | flops 201326592 | bytes 151257088 | tf_op jit(solution)/shard_map/transpose | solution.py:69
  128.2 15.5 copy.28
  143.7 21.4 %convolution_bitcast_fusion = f32[64,8,128,128]{3,2,1,0:T(8,128)} fusion(bf16[64,8,128,128]{3,2,1,0:T(8,128)(2,1)} %bitcast.71, bf16[64,64]{1,0:T(8,128)(2,1)S(1)} %get-tuple-element.22, bf16[64,64]{1,0:T(8,128)(2,1)S(1)} %get-tuple-element.21, bf16[64,64]{1,0:T(8,128)(2,1)S(1)} %fusion.72), kind=kOutput, calls=%fused_computation.21 | convolution fusion | flops 2147614720 | bytes 50356224 | tf_op jit(solution)/shard_map/km,ismq->iskq/dot_general | solution.py:72
  165.1 15.0 subtract_convert_fusion.1
  180.1 14.9 fusion.11
  195.0 21.8 %fusion.80 = (f32[64,8,128,64]{2,3,1,0:T(8,128)}, f32[64,8,128,64]{2,3,1,0:T(8,128)}) fusion(f32[64,8,256,64]{2,3,1,0:T(8,128)} %fusion.11), kind=kLoop, calls=%fused_computation.131 | loop fusion | bytes 67108864 | tf_op jit(solution)/shard_map/slice | solution.py:80
  216.7 22.9 %copy.29 = f32[64,8,128,64]{3,2,1,0:T(8,128)} copy(f32[64,8,128,64]{2,3,1,0:T(8,128)} %get-tuple-element.9) | data formatting | bytes 33554432 | tf_op jit(solution)/shard_map/slice | solution.py:80
  239.6 27.9 %reshape.235 = f32[1,64,8,32,256]{4,3,2,1,0:T(8,128)} reshape(f32[64,8,128,64]{3,2,1,0:T(8,128)} %copy.29) | data formatting | bytes 33554432 | tf_op jit(solution)/shard_map/reshape | solution.py:80
  267.5 22.9 %copy.31 = f32[64,8,128,64]{3,2,1,0:T(8,128)} copy(f32[64,8,128,64]{2,3,1,0:T(8,128)} %get-tuple-element.10) | data formatting | bytes 33554432 | tf_op jit(solution)/shard_map/slice | solution.py:81
  290.4 28.4 %reshape.236 = f32[1,64,8,32,256]{4,3,2,1,0:T(8,128)} reshape(f32[64,8,128,64]{3,2,1,0:T(8,128)} %copy.31) | data formatting | bytes 33554432 | tf_op jit(solution)/shard_map/reshape | solution.py:81
  318.8 2.6 slice_multiply_fusion.1
  322.7 34.0 %subtract_convert_fusion = (bf16[1,64,8,32,256]{4,2,3,1,0:T(8,128)(2,1)S(1)}, bf16[1,64,8,32,256]{4,2,3,1,0:T(8,128)(2,1)}) fusion(f32[1,64,8,32,256]{4,3,2,1,0:T(8,128)} %reshape.236, f32[1,64,8,32,256]{4,3,2,1,0:T(8,128)} %reshape.235, f32[64,32,256]{2,1,0:T(8,128)S(1)} %bitcast.76, f32[64,32,256]{2,1,0:T(8,128)S(1)} %bitcast.75), kind=kLoop, calls=%fused_computation.17 | loop fusion | flops 33554432 | bytes 54525952 | tf_op jit(solution)/shard_map/convert.5
  356.7 10.5 pad_maximum_fusion
  367.2 13.9 gather_fusion.1
  381.2 14.2 select_bitcast_fusion
  395.3 7.5 all-to-all-start
  405.6 361.7 %all-to-all-done = bf16[2,64,8,32,256]{4,2,1,0,3:T(8,128)(2,1)} async-done(((bf16[2,64,8,32,256]{4,2,1,0,3:T(8,128)(2,1)}), bf16[2,64,8,32,256]{4,2,1,0,3:T(8,128)(2,1)}, u32[]{:S(2)}, u32[]{:S(2)}) %all-to-all-start) | async-done | bytes 16777248 | tf_op jit(solution)/shard_map/all_to_all | solution.py:119
  767.3 13.7 copy.35
  781.0 26.2 %copy.36 = bf16[2,2048,8,256]{1,2,0,3:T(8,128)(2,1)} copy(bf16[2,2048,8,256]{3,2,1,0:T(8,128)(2,1)} %bitcast.72) | data formatting | bytes 33554432 | tf_op jit(solution)/shard_map/squeeze | solution.py:119
  807.2 444.7 %fusion.4 = f32[256,64,2,8]{1,3,2,0:T(8,128)S(1)} fusion(bf16[2,2048,8,256]{1,2,0,3:T(8,128)(2,1)} %copy.36, f32[64,2048]{1,0:T(8,128)S(1)} %broadcast_select_fusion, f32[256]{0:T(256)S(1)} %add_convert_fusion.3), kind=kOutput, calls=%fused_computation.8 | convolution fusion | flops 1207959552 | bytes 18351104 | tf_op jit(solution)/shard_map/cbi,pisc->cbps/dot_general | solution.py:122
  1251.9 449.0 %fusion.2 = f32[256,64,2,8]{1,3,2,0:T(8,128)S(1)} fusion(bf16[2,2048,8,256]{1,2,0,3:T(8,128)(2,1)S(1)} %copy-done.1, f32[64,2048]{1,0:T(8,128)S(1)} %broadcast_select_fusion, f32[256]{0:T(256)S(1)} %add_convert_fusion.3), kind=kOutput, calls=%fused_computation.7 | convolution fusion | flops 1207959552 | bytes 18351104 | tf_op jit(solution)/shard_map/cbi,pisc->cbps/dot_general | solution.py:123
  1702.9 9.1 all_to_all.24
  (38 shorter events, 10.6 us)
Async XLA Ops:
  0.0 404.7 %copy-start = (f32[64,2048]{1,0:T(8,128)S(1)}, f32[64,2048]{1,0:T(8,128)}, u32[]{:S(2)}) copy-start(f32[64,2048]{1,0:T(8,128)} %param.7) | copy-start | bytes 1572868
  318.8 3.9 copy-start.3
  318.8 3.9 copy-start.2
  395.3 9.4 copy-start.4
  395.3 372.0 %all-to-all-start = ((bf16[2,64,8,32,256]{4,2,1,0,3:T(8,128)(2,1)}), bf16[2,64,8,32,256]{4,2,1,0,3:T(8,128)(2,1)}, u32[]{:S(2)}, u32[]{:S(2)}) async-start(bf16[2,64,8,32,256]{4,2,1,0,3:T(8,128)(2,1)} %select_bitcast_fusion), calls=%async_computation | async-start | bytes 33554432 | tf_op jit(solution)/shard_map/all_to_all | solution.py:119
  807.2 444.7 %copy-start.1 = (bf16[2,2048,8,256]{1,2,0,3:T(8,128)(2,1)S(1)}, bf16[2,2048,8,256]{1,2,0,3:T(8,128)(2,1)}, u32[]{:S(2)}) copy-start(bf16[2,2048,8,256]{1,2,0,3:T(8,128)(2,1)} %copy.36) | copy-start | bytes 50331652
where the time goes:
time: 1730 us; the launch traced here: 1710 us
  matrix products  930 us (54%)
  waiting for transfers between devices  362 us (21%)
  local copies, waits for them, and re-layouts  235 us (14%)
  other arithmetic  168 us (10%)
    dot_general x1, matrix products, body(): jnp.einsum('cbi,pisc->cbps', weight_imag, piece, preferred_element_type=j...  449 us
    dot_general x1, matrix products, body(): jnp.einsum('cbi,pisc->cbps', weight_real, piece, preferred_element_type=j...  445 us
    all_to_all x1, waiting for transfers between devices, body(): lax.all_to_all(blocks, ('gx', 'gy'), split_axis=3, concat_axis=1, tiled=T...  362 us
    transpose x1, other arithmetic, transform(): jnp.transpose(filtered.reshape(2, inputs_here, spectra_here, first_len, s...  85.1 us
    another operation x6, other arithmetic  49.9 us
    slice x2, local copies, waits for them, and re-layouts, transform(): outer[:, :, :second_len].reshape(inputs_here, spectra_here, NCH) * scale  44.6 us
    reshape x1, local copies, waits for them, and re-layouts, body(): frames = voltages.reshape(2, inputs_here, NSPEC + TAPS - 1, NCH)  36.2 us
  transfers between devices with their start and end apart: 1, of which 1 were waited for; matrix products, arithmetic and copies ran while one was open for 0% of the time, Pallas kernels for 0%

commit v1 on v0

--- a/solution.py
+++ b/solution.py
@@ -1,8 +1,11 @@
+import functools
 import math
 
 import jax
 import jax.numpy as jnp
 from jax import lax
+from jax.experimental import pallas as pl
+from jax.experimental.pallas import tpu as pltpu
 from jax.sharding import PartitionSpec as P
 
 NIN = 2048
@@ -12,6 +15,9 @@
 INTEG = 2
 NSPEC = 8
 TIMES = 4
+SLOT = 64
+RUN = 64
+COARSE = 16
 
 
 def coefficients():
@@ -82,13 +88,8 @@
     return (outer_real, outer_imag)
 
 
-def body(voltages, gains, delays, channel_order, beam_table):
-    across = lax.axis_size("gx")
-    along = lax.axis_size("gy")
-    devices = across * along
+def spectra_of(voltages, gains):
     inputs_here = voltages.shape[1]
-    width = NCH // devices
-    beams_here = NBEAM // along
     frames = voltages.reshape(2, inputs_here, NSPEC + TAPS - 1, NCH)
     taps_table = coefficients()
     filtered = taps_table[0] * frames[:, :, 0:NSPEC].astype(jnp.float32)
@@ -105,36 +106,192 @@
             gain_real * spec_imag + gain_imag * spec_real,
         ]
     ).astype(jnp.bfloat16)
-    order = (jnp.arange(across, dtype=jnp.int32)[:, None] * along + channel_order).reshape(-1)
-    blocks = jnp.take(calibrated.reshape(2, inputs_here, NSPEC, devices, width), order, axis=3)
+    arranged = jnp.transpose(calibrated, (3, 2, 0, 1))
+    if inputs_here < SLOT:
+        arranged = jnp.pad(arranged, ((0, 0), (0, 0), (0, 0), (0, SLOT - inputs_here)))
+    return arranged.reshape(NCH, NSPEC, 2 * SLOT)
+
+
+def phase_tables(offsets):
+    turn = offsets * (2.0 * math.pi / NCH)
+    both = jnp.concatenate([turn, turn], axis=1)
+    fine = jnp.arange(RUN, dtype=jnp.float32)[:, None, None] * both[None]
+    steps = NCH // RUN // COARSE
+    middle = (RUN * jnp.arange(COARSE, dtype=jnp.float32))[:, None, None] * both[None]
+    wide = (RUN * COARSE * jnp.arange(steps, dtype=jnp.float32))[:, None, None] * turn[None]
+    wide_cos = jnp.cos(wide)
+    wide_sin = jnp.sin(wide)
+    scale = NIN ** (-0.5)
+    return (
+        jnp.stack([jnp.cos(fine), jnp.sin(fine)]),
+        jnp.stack([jnp.cos(middle), jnp.sin(middle)]),
+        jnp.stack(
+            [
+                jnp.concatenate([wide_cos, wide_sin], axis=2) * scale,
+                jnp.concatenate([wide_sin, -wide_cos], axis=2) * scale,
+            ]
+        ),
+    )
+
+
+def beam_kernel(spectra, fine, middle, wide, out):
+    step = pl.program_id(0)
+    lanes = 2 * SLOT
+    bases = []
+    for half in range(2):
+        run = 2 * step + half
+        coarse = run // COARSE
+        rest = run % COARSE
+        wide_cos = wide[0, coarse]
+        wide_sin = wide[1, coarse]
+        middle_cos = middle[0, rest]
+        middle_sin = middle[1, rest]
+        bases.append(
+            (
+                wide_cos * middle_cos - wide_sin * middle_sin,
+                wide_sin * middle_cos + wide_cos * middle_sin,
+            )
+        )
+    lane = lax.broadcasted_iota(jnp.int32, (NBEAM, 2 * lanes), 1)
+    member = (lane // NSPEC) % 8
+    sign = jnp.where(
+        lax.broadcasted_iota(jnp.int32, (8 * NSPEC, lanes), 1) < SLOT, 1.0, -1.0
+    ).astype(jnp.float32)
+    blank = jnp.zeros((16 * NSPEC, lanes), jnp.bfloat16)
+
+    def group(index):
+        rights = []
+        for half in range(2):
+            block = spectra[half, pl.ds(index * 8, 8)].reshape(8 * NSPEC, lanes)
+            swapped = (pltpu.roll(block.astype(jnp.float32), SLOT, 1) * sign).astype(jnp.bfloat16)
+            rights.append(jnp.concatenate([block, swapped], axis=0))
+        right = jnp.concatenate(
+            [
+                jnp.concatenate([rights[0], blank], axis=1),
+                jnp.concatenate([blank, rights[1]], axis=1),
+            ],
+            axis=0,
+        )
+        lefts = []
+        for inner in range(8):
+            fine_cos = fine[0, index * 8 + inner]
+            fine_sin = fine[1, index * 8 + inner]
+            lefts.append(
+                jnp.concatenate(
+                    [
+                        (base_cos * fine_cos - base_sin * fine_sin).astype(jnp.bfloat16)
+                        for base_cos, base_sin in bases
+                    ],
+                    axis=1,
+                )
+            )
+        products = lax.dot_general(
+            jnp.concatenate(lefts, axis=0),
+            right,
+            (((1,), (1,)), ((), ())),
+            preferred_element_type=jnp.float32,
+        )
+        total = products[:NBEAM]
+        for inner in range(1, 8):
+            total = jnp.where(
+                member == inner, products[inner * NBEAM : (inner + 1) * NBEAM], total
+            )
+        return total
+
+    def pair(index, carry):
+        low = group(2 * index)
+        high = group(2 * index + 1)
+        for unit in range(8):
+            rows = slice(unit * 8, unit * 8 + 8)
+            both = jnp.concatenate([low[rows], high[rows]], axis=0).astype(jnp.bfloat16)
+            out[unit % 2, 0, unit // 2, pl.ds(index * 16, 16), :] = both
+        return carry
+
+    lax.fori_loop(0, RUN // 16, pair, 0)
+
+
+def partial_beams(spectra, tables):
+    runs = NCH // (2 * RUN)
+    fine, middle, wide = tables
+    whole = lambda array: pl.BlockSpec(array.shape, lambda step: (0,) * array.ndim)
+    return pl.pallas_call(
+        beam_kernel,
+        grid=(runs,),
+        in_specs=[
+            pl.BlockSpec((2, RUN, NSPEC, 2 * SLOT), lambda step: (step, 0, 0, 0)),
+            whole(fine),
+            whole(middle),
+            whole(wide),
+        ],
+        out_specs=pl.BlockSpec((2, 1, 4, RUN, 4 * SLOT), lambda step: (0, step, 0, 0, 0)),
+        out_shape=jax.ShapeDtypeStruct((2, runs, 4, RUN, 4 * SLOT), jnp.bfloat16),
+        compiler_params=pltpu.CompilerParams(
+            dimension_semantics=("arbitrary",), vmem_limit_bytes=48 * 1024 * 1024
+        ),
+        name="beam_sums",
+    )(spectra.reshape(NCH // RUN, RUN, NSPEC, 2 * SLOT), fine, middle, wide)
+
+
+def detect(beams):
+    runs, groups, count, lanes = beams.shape
+    wide = beams.astype(jnp.float32)
+    source = jnp.arange(lanes, dtype=jnp.int32)
+    source_half = source // (16 * NSPEC)
+    source_channel = source // NSPEC % 8
+    source_time = source % NSPEC // INTEG
+    place = (source_half * TIMES + source_time) * 8 + source_channel
+    pick = (place[:, None] == jnp.arange(2 * TIMES * 8, dtype=jnp.int32)[None]).astype(jnp.float32)
+    power = jnp.einsum(
+        "tgrl,lm->tgrm",
+        wide * wide,
+        pick,
+        precision=lax.Precision.HIGHEST,
+        preferred_element_type=jnp.float32,
+    )
+    power = power.reshape(runs, groups, count, 2, TIMES, 8)
+    return jnp.transpose(power, (2, 4, 0, 3, 1, 5)).reshape(count, TIMES, runs * 2 * groups * 8)
+
+
+def body(voltages, gains, delays, channel_order, beam_table):
+    across = lax.axis_size("gx")
+    along = lax.axis_size("gy")
+    inputs_here = voltages.shape[1]
+    beams_here = NBEAM // along
     column = lax.axis_index("gx")
     member = lax.axis_index("gy")
-    owned = column * along + channel_order[column, member]
-    channel = (owned * width + jnp.arange(width, dtype=jnp.int32)).astype(jnp.float32)
-    offsets = jnp.take(delays, beam_table, axis=0)
-    phase = channel[:, None, None] * offsets[None] * (-2.0 * math.pi / NCH)
-    scale = NIN ** (-0.5)
-    weight_real = (jnp.cos(phase) * scale).astype(jnp.bfloat16)
-    weight_imag = (jnp.sin(phase) * scale).astype(jnp.bfloat16)
-    piece = lax.all_to_all(blocks, ("gx", "gy"), split_axis=3, concat_axis=1, tiled=True)[
-        :, :, :, 0, :
-    ]
-    first = jnp.einsum("cbi,pisc->cbps", weight_real, piece, preferred_element_type=jnp.float32)
-    second = jnp.einsum("cbi,pisc->cbps", weight_imag, piece, preferred_element_type=jnp.float32)
-    beam_real = (first[:, :, 0] - second[:, :, 1]).astype(jnp.bfloat16)
-    beam_imag = (first[:, :, 1] + second[:, :, 0]).astype(jnp.bfloat16)
-    voltage_beams = jnp.stack([beam_real, beam_imag], axis=2)
-    local_real = voltage_beams[:, :, 0].astype(jnp.float32)
-    local_imag = voltage_beams[:, :, 1].astype(jnp.float32)
-    local_power = (
-        (local_real * local_real + local_imag * local_imag)
-        .reshape(width, NBEAM, TIMES, INTEG)
-        .sum(axis=3)
-    )
-    power = lax.all_to_all(
-        local_power[None].astype(jnp.bfloat16), "gy", split_axis=2, concat_axis=0, tiled=True
-    ).astype(jnp.float32)
-    return jnp.transpose(power, (2, 3, 0, 1)).reshape(beams_here, TIMES, along * width)
+    first_input = (column * along + member) * inputs_here
+    offsets = jnp.take(
+        lax.dynamic_slice_in_dim(delays, first_input, inputs_here, 1), beam_table, axis=0
+    )
+    if inputs_here < SLOT:
+        offsets = jnp.pad(offsets, ((0, 0), (0, SLOT - inputs_here)))
+    spectra = spectra_of(voltages, gains)
+    partial = partial_beams(spectra, phase_tables(offsets))
+    runs = partial.shape[1]
+    groups = RUN // 8
+    lanes = 4 * SLOT
+    pairs = [[2 * index, 2 * index + 1] for index in range(along // 2)]
+    evens = [[2 * index + odd for index in range(along // 2)] for odd in range(2)]
+    if beams_here != 8:
+        partial = jnp.transpose(
+            partial.reshape(2, runs, 4, groups, 8, lanes), (2, 0, 4, 1, 3, 5)
+        ).reshape(along // 2, 2, beams_here, runs, groups, lanes)
+        partial = jnp.transpose(partial, (1, 3, 0, 4, 2, 5)).reshape(
+            2, runs, along // 2, groups * beams_here, lanes
+        )
+    halves = lax.all_to_all(partial, "gy", 0, 0, tiled=True, axis_index_groups=pairs)
+    chip = (halves[0].astype(jnp.float32) + halves[1].astype(jnp.float32)).astype(jnp.bfloat16)
+    column_sum = lax.psum_scatter(chip, "gx", scatter_dimension=0, tiled=True)
+    swapped = jnp.transpose(column_sum, (1, 0, 2, 3))
+    beams = lax.psum_scatter(
+        swapped, "gy", scatter_dimension=0, axis_index_groups=evens, tiled=True
+    )
+    power = detect(beams.reshape(runs // across, groups, beams_here, lanes))
+    width = NCH // (across * along)
+    order = channel_order[column]
+    return jnp.take(power.reshape(beams_here, TIMES, along, width), order, axis=2).reshape(
+        beams_here, TIMES, along * width
+    )
 
 
 def solution(mesh):

time: 1730 us -> 806 us (0.47)
  matrix products: 930 us -> 39.8 us
  waiting for transfers between devices: 362 us -> 177 us
  Pallas kernels: 0 us -> 110 us
  local copies, waits for them, and re-layouts: 235 us -> 280 us
    dot_general x2 -> x1, matrix products: 894 us -> 3.57 us  [detect(): jnp.einsum('tgrl,lm->tgrm', wide * wide, pick, precision=lax.Precision.HI...]
    all_to_all x1 -> x0, waiting for transfers between devices: 362 us -> none  [body(): lax.all_to_all(blocks, ('gx', 'gy'), split_axis=3, concat_axis=1, tiled=T...]
    pallas_call x0 -> x1, Pallas kernels: none -> 110 us  [partial_beams(): pl.pallas_call(beam_kernel, grid=(runs,), in_specs=[pl.BlockSpec((2, RUN,...]
    another operation x0 -> x4, local copies, waits for them, and re-layouts: none -> 97.9 us  [the longest x2 93.7 us: partial_beams(): spectra.reshape(NCH // RUN, RUN, NSPEC, 2 * SLOT)]
    reduce_scatter x0 -> x1, waiting for transfers between devices: none -> 89.1 us  [body(): column_sum = lax.psum_scatter(chip, 'gx', scatter_dimension=0, tiled=True)]
    unnamed x0 -> x3, waiting for transfers between devices: none -> 87.8 us
    another operation x7 -> x9, other arithmetic: 60.3 us -> 31.3 us
    squeeze x1 -> x0, local copies, waits for them, and re-layouts: 26.2 us -> none  [body(): lax.all_to_all(blocks, ('gx', 'gy'), split_axis=3, concat_axis=1, tiled=T...]
  transfers between devices with their start and end apart: 1 -> 2, of which waited for: 1 -> 2; matrix products, arithmetic and copies ran while one was open for 0% -> 0% of each run, Pallas kernels for 0% -> 0%
where the time goes in v1:
time: 806 us; the launch traced here: 794 us
  local copies, waits for them, and re-layouts  280 us (35%)
  waiting for transfers between devices  177 us (22%)
  other arithmetic  152 us (19%)
  Pallas kernels  110 us (14%)
  matrix products  39.8 us (5%)
  blocking collectives  19.5 us (2%)
  between operations  14.8 us (2%)
    pallas_call x1, Pallas kernels, partial_beams(): pl.pallas_call(beam_kernel, grid=(runs,), in_specs=[pl.BlockSpec((2, RUN,...  110 us
    another operation x2, local copies, waits for them, and re-layouts, partial_beams(): spectra.reshape(NCH // RUN, RUN, NSPEC, 2 * SLOT)  93.7 us
    reduce_scatter x1, waiting for transfers between devices, body(): column_sum = lax.psum_scatter(chip, 'gx', scatter_dimension=0, tiled=True)  89.1 us
    unnamed x3, waiting for transfers between devices  87.8 us
    transpose x1, other arithmetic, transform(): jnp.transpose(filtered.reshape(2, inputs_here, spectra_here, first_len, s...  85.1 us
    slice x2, local copies, waits for them, and re-layouts, transform(): outer[:, :, second_len:].reshape(inputs_here, spectra_here, NCH) * scale  44.6 us
    reshape x1, local copies, waits for them, and re-layouts, spectra_of(): frames = voltages.reshape(2, inputs_here, NSPEC + TAPS - 1, NCH)  36.2 us
    another operation x6, other arithmetic  30.9 us
  transfers between devices with their start and end apart: 2, of which 2 were waited for; matrix products, arithmetic and copies ran while one was open for 0% of the time, Pallas kernels for 0%

profile of v1, /device:TPU:0, one launch (start us, length us, event | category | flops | bytes accessed | tf_op | source)
XLA Modules:
  0.0 793.9 jit_solution(14805207840392073765)
XLA Ops:
  14.9 36.2 %reshape.323 = bf16[2,64,15,8192]{3,2,1,0:T(8,128)(2,1)} reshape(bf16[2,64,122880]{2,1,0:T(8,128)(2,1)} %param.5) | data formatting | bytes 62914560 | tf_op jit(solution)/shard_map/reshape | solution.py:93
  51.1 85.1 %fusion.4 = bf16[64,8,2,64,128]{4,1,3,0,2:T(8,128)(2,1)} fusion(bf16[2,64,15,8192]{3,2,1,0:T(8,128)(2,1)} %reshape.323, f32[8192]{0:T(1024)S(1)} %get-tuple-element.16, f32[8192]{0:T(1024)S(1)} %get-tuple-element.17, f32[8192]{0:T(1024)S(1)} %get-tuple-element.18, f32[8192]{0:T(1024)S(1)} %get-tuple-element.19, f32[8192]{0:T(1024)S(1)} %get-tuple-element.20, ...), kind=kLoop, calls=%fused_computation.13 | loop fusion | flops 201326592 | bytes 151257088 | tf_op jit(solution)/shard_map/transpose | solution.py:75
  136.3 15.4 %copy.25 = bf16[64,8,2,64,128]{4,3,2,1,0:T(8,128)(2,1)} copy(bf16[64,8,2,64,128]{4,1,3,0,2:T(8,128)(2,1)} %fusion.4) | data formatting | bytes 33554432 | tf_op jit(solution)/shard_map/transpose | solution.py:75
  151.7 21.4 %convolution_bitcast_fusion = f32[64,8,128,128]{3,2,1,0:T(8,128)} fusion(bf16[64,8,128,128]{3,2,1,0:T(8,128)(2,1)} %bitcast.75, bf16[64,64]{1,0:T(8,128)(2,1)S(1)} %get-tuple-element.31, bf16[64,64]{1,0:T(8,128)(2,1)S(1)} %get-tuple-element.30, bf16[64,64]{1,0:T(8,128)(2,1)S(1)} %fusion.79), kind=kOutput, calls=%fused_computation.14 | convolution fusion | flops 2147614720 | bytes 50356224 | tf_op jit(solution)/shard_map/km,ismq->iskq/dot_general | solution.py:78
  173.1 15.0 %subtract_convert_fusion.1 = (bf16[64,8,64,128]{3,2,1,0:T(8,128)(2,1)S(1)}, bf16[64,8,64,128]{3,2,1,0:T(8,128)(2,1)}) fusion(f32[64,8,128,128]{3,2,1,0:T(8,128)} %convolution_bitcast_fusion, f32[64,128]{1,0:T(8,128)S(1)} %get-tuple-element.32, f32[64,128]{1,0:T(8,128)S(1)} %get-tuple-element.33), kind=kLoop, calls=%fused_computation.12 | loop fusion | flops 33554432 | bytes 50397184 | tf_op jit(solution)/shard_map/convert.2
  188.1 14.9 %fusion.5 = f32[64,8,256,64]{2,3,1,0:T(8,128)} fusion(bf16[64,8,64,128]{3,2,1,0:T(8,128)(2,1)} %get-tuple-element.8, bf16[64,8,64,128]{3,2,1,0:T(8,128)(2,1)S(1)} %get-tuple-element.7, bf16[128,128]{1,0:T(8,128)(2,1)S(1)} %get-tuple-element.35, bf16[128,128]{1,0:T(8,128)(2,1)S(1)} %fusion.76, bf16[128,128]{1,0:T(8,128)(2,1)S(1)} %get-tuple-element.34), kind=kOutput, calls=%fused_computation.15 | convolution fusion | flops 4329046016 | bytes 50429952 | tf_op jit(solution)/shard_map/iskq,qn->isnk/dot_general | solution.py:84
  203.0 21.8 %fusion.92 = (f32[64,8,128,64]{2,3,1,0:T(8,128)}, f32[64,8,128,64]{2,3,1,0:T(8,128)}) fusion(f32[64,8,256,64]{2,3,1,0:T(8,128)} %fusion.5), kind=kLoop, calls=%fused_computation.167 | loop fusion | bytes 67108864 | tf_op jit(solution)/shard_map/slice | solution.py:87
  224.8 22.9 %copy.26 = f32[64,8,128,64]{3,2,1,0:T(8,128)} copy(f32[64,8,128,64]{2,3,1,0:T(8,128)} %get-tuple-element.10) | data formatting | bytes 33554432 | tf_op jit(solution)/shard_map/slice | solution.py:86
  247.7 27.9 %reshape.326 = f32[1,64,8,8192]{3,2,1,0:T(8,128)} reshape(f32[64,8,128,64]{3,2,1,0:T(8,128)} %copy.26) | data formatting | bytes 33554432 | tf_op jit(solution)/shard_map/reshape | solution.py:86
  275.6 22.9 %copy.27 = f32[64,8,128,64]{3,2,1,0:T(8,128)} copy(f32[64,8,128,64]{2,3,1,0:T(8,128)} %get-tuple-element.9) | data formatting | bytes 33554432 | tf_op jit(solution)/shard_map/slice | solution.py:87
  298.4 27.9 %reshape.327 = f32[1,64,8,8192]{3,2,1,0:T(8,128)} reshape(f32[64,8,128,64]{3,2,1,0:T(8,128)} %copy.27) | data formatting | bytes 33554432 | tf_op jit(solution)/shard_map/reshape | solution.py:87
  329.1 15.0 %subtract_convert_fusion = (bf16[1,64,8,8192]{3,2,1,0:T(8,128)(2,1)S(1)}, bf16[1,64,8,8192]{3,2,1,0:T(8,128)(2,1)}) fusion(f32[1,64,8,8192]{3,2,1,0:T(8,128)} %reshape.327, f32[1,64,8,8192]{3,2,1,0:T(8,128)} %reshape.326, f32[64,8192]{1,0:T(8,128)S(1)} %get-tuple-element.12, f32[64,8192]{1,0:T(8,128)S(1)} %get-tuple-element.11), kind=kLoop, calls=%fused_computation.10 | loop fusion | flops 33554432 | bytes 54525952 | tf_op jit(solution)/shard_map/convert
  344.1 10.5 %maximum_bitcast_fusion = bf16[8192,8,2,64]{0,1,3,2:T(8,128)(2,1)} fusion(bf16[1,64,8,8192]{3,2,1,0:T(8,128)(2,1)} %get-tuple-element.6, bf16[1,64,8,8192]{3,2,1,0:T(8,128)(2,1)S(1)} %get-tuple-element.5), kind=kLoop, calls=%fused_computation.7 | loop fusion | flops 8388608 | bytes 33554432 | tf_op jit(solution)/shard_map/transpose | solution.py:109
  354.6 46.0 %reshape.349 = bf16[128,64,8,128]{1,0,2,3:T(8,128)(2,1)} reshape(bf16[8192,8,2,64]{0,1,3,2:T(8,128)(2,1)} %maximum_bitcast_fusion) | data formatting | bytes 33554432 | tf_op jit(solution)/shard_map/reshape;reshape | solution.py:232
  400.6 47.7 %copy.29.spectra = bf16[128,64,8,128]{3,2,1,0:T(8,128)(2,1)} copy(bf16[128,64,8,128]{1,0,2,3:T(8,128)(2,1)} %reshape.349) | data formatting | bytes 33554432 | tf_op jit(solution)/shard_map/reshape;reshape | solution.py:232
  450.2 7.2 fusion.10
  460.0 110.5 %beam_sums.1 = bf16[2,64,4,64,256]{4,3,2,1,0:T(8,128)(2,1)} custom-call(bf16[128,64,8,128]{3,2,1,0:T(8,128)(2,1)} %copy.29.spectra, f32[2,64,64,128]{3,2,1,0:T(8,128)S(1)} %pad_maximum_fusion.fine, f32[2,16,64,128]{3,2,1,0:T(8,128)S(1)} %pad_maximum_fusion.1.middle, f32[2,8,64,128]{3,2,1,0:T(8,128)S(1)} %pad_maximum_fusion.2.wide), custom_call_target="tpu_custom_call" | custom-call | tf_op jit(solution)/shard_map/beam_sums/pallas_call | solution.py:217
  570.5 19.5 %all_to_all.5 = bf16[2,64,4,64,256]{4,3,2,1,0:T(8,128)(2,1)S(1)} all-to-all(bf16[2,64,4,64,256]{4,3,2,1,0:T(8,128)(2,1)} %beam_sums.1), channel_id=1, replica_groups={{0,1},{2,3},{4,5},{6,7},{8,9},{10,11},{12,13},{14,15},{16,17},{18,19},{..., dimensions={0} | all-to-all | bytes 33554432 | tf_op jit(solution)/shard_map/all_to_all | solution.py:282
  590.0 5.2 fusion.8
  595.3 89.1 %reduce-scatter.5.cloned.1.call-done = bf16[16,4,64,256]{3,2,1,0:T(8,128)(2,1)} async-done(((bf16[64,4,64,256]{3,2,1,0:T(8,128)(2,1)}), bf16[16,4,64,256]{3,2,1,0:T(8,128)(2,1)}) %reduce-scatter.5.cloned.1.call-update) | async-done | bytes 2097168 | tf_op jit(solution)/shard_map/reduce_scatter | solution.py:284
  685.2 87.7 %all-reduce.3.cloned.1.call-done = bf16[4,16,64,256]{3,2,0,1:T(8,128)(2,1)} async-done(((bf16[4,16,64,256]{3,2,0,1:T(8,128)(2,1)}), bf16[4,16,64,256]{3,2,0,1:T(8,128)(2,1)}) %all-reduce.3.cloned.1.call-update) | async-done | bytes 2097168
  773.0 3.6 convolution_bitcast_fusion.1
  776.5 4.4 copy.30
  780.9 4.0 reshape_reshape.7
  (55 shorter events, 17.1 us)
Async XLA Ops:
  6.5 441.8 %copy-start = (f32[64,2048]{1,0:T(8,128)S(1)}, f32[64,2048]{1,0:T(8,128)}, u32[]{:S(2)}) copy-start(f32[64,2048]{1,0:T(8,128)} %param.7) | copy-start | bytes 1572868
  6.5 677.9 %reduce-scatter.5.cloned.1.call-start = ((), (), s32[]{:S(2)}) async-start(), calls=%async_computation.2 | async-start | bytes 10485760 | tf_op jit(solution)/shard_map/reduce_scatter | solution.py:284
  400.6 47.7 %copy-start.3 = (s32[64]{0:T(128)S(1)}, s32[64]{0:T(128)}, u32[]{:S(2)}) copy-start(s32[64]{0:T(128)} %compare_select_fusion.1) | copy-start | bytes 772
  400.6 48.4 %copy-start.2 = (pred[64]{0:T(512)(128)(4,1)S(1)}, pred[64]{0:T(512)(128)(4,1)}, u32[]{:S(2)}) copy-start(pred[64]{0:T(512)(128)(4,1)} %compare_and_fusion) | copy-start | bytes 196
  400.6 48.6 %copy-start.4 = (f32[8]{0:T(128)S(1)}, f32[8]{0:T(128)}, u32[]{:S(2)}) copy-start(f32[8]{0:T(128)} %iota_multiply_fusion.2) | copy-start | bytes 100
  400.6 56.8 %copy-start.1 = (f32[16]{0:T(128)S(1)}, f32[16]{0:T(128)}, u32[]{:S(2)}) copy-start(f32[16]{0:T(128)} %iota_multiply_fusion.3) | copy-start | bytes 196
  590.0 94.5 %copy-start.5 = (s32[4,8]{1,0:T(4,128)S(1)}, s32[4,8]{1,0:T(4,128)}, u32[]{:S(2)}) copy-start(s32[4,8]{1,0:T(4,128)} %param.8) | copy-start | bytes 388
  590.0 94.6 %copy-start.6 = (u32[32]{0:T(128)S(1)}, u32[32]{0:T(128)}, u32[]{:S(2)}) copy-start(u32[32]{0:T(128)} %constant.197) | copy-start | bytes 388
  595.3 177.7 %all-reduce.3.cloned.1.call-start = ((), (), s32[]{:S(2)}) async-start(), calls=%async_computation.3 | async-start | bytes 4194304
Sparse Core Ops, SparseCore 0:
  595.4 88.9 reduce-scatter.4
  686.8 86.1 all-reduce.2

commit v2 on v1

v2 whole, which is shorter than its diff:
```python
import functools
import math

import jax
import jax.numpy as jnp
from jax import lax
from jax.experimental import pallas as pl
from jax.experimental.pallas import tpu as pltpu
from jax.sharding import PartitionSpec as P

NIN = 2048
NCH = 8192
NBEAM = 64
TAPS = 8
INTEG = 2
NSPEC = 8
TIMES = 4
CHUNKS = 2
PITCH = 24
SLOT = 64
FIRST = 64
RUN = 64


def coefficients():
    total = TAPS * NCH
    index = jnp.arange(total, dtype=jnp.float32)
    offset = (index - total / 2) / NCH
    window = 0.5 - 0.5 * jnp.cos(2.0 * math.pi * index / total)
    raw = jnp.sinc(offset) * window
    raw = raw / jnp.sqrt(jnp.sum(raw * raw) / NCH)
    return raw.reshape(TAPS, NCH)


def combine_tables():
    second_len = NCH // FIRST
    first_ids = jnp.arange(FIRST, dtype=jnp.int32)
    second_ids = jnp.arange(second_len, dtype=jnp.int32)
    small = (2.0 * math.pi / FIRST) * (
        first_ids[:, None] * first_ids[None, :] % FIRST
    ).astype(jnp.float32)
    twist = (2.0 * math.pi / NCH) * (second_ids[:, None] * first_ids[None, :]).astype(jnp.float32)
    small_cos, small_sin = jnp.cos(small)[None], jnp.sin(small)[None]
    twist_cos, twist_sin = jnp.cos(twist)[:, :, None], jnp.sin(twist)[:, :, None]
    first = jnp.concatenate(
        [
            small_cos * twist_cos - small_sin * twist_sin,
            -(small_sin * twist_cos + small_cos * twist_sin),
        ],
        axis=2,
    ).astype(jnp.bfloat16)
    large = (2.0 * math.pi / second_len) * (
        second_ids[:, None] * second_ids[None, :] % second_len
    ).astype(jnp.float32)
    second = jnp.concatenate([jnp.cos(large), -jnp.sin(large)], axis=1).astype(jnp.bfloat16)
    return first, second


def filter_kernel(*refs):
    frames = refs[: NSPEC + TAPS - 1]
    taps = refs[NSPEC + TAPS - 1]
    out = refs[NSPEC + TAPS]
    inputs_here = frames[0].shape[1]
    for piece in range(out.shape[1]):
        lanes = slice(piece * 128, piece * 128 + 128)
        for spectrum in range(NSPEC):
            parts = []
            for part in range(2):
                total = taps[0:1, lanes] * frames[spectrum][part, :, lanes].astype(jnp.float32)
                for tap in range(1, TAPS):
                    total = total + taps[tap : tap + 1, lanes] * frames[spectrum + tap][
                        part, :, lanes
                    ].astype(jnp.float32)
                parts.append(total)
                if inputs_here < SLOT:
                    parts.append(jnp.zeros((SLOT - inputs_here, 128), jnp.float32))
            rows = jnp.concatenate(parts, axis=0)
            out[spectrum, piece] = jnp.transpose(rows).astype(jnp.bfloat16)


def quarter_turn(rows, sign):
    return pltpu.roll(rows, SLOT, 1) * sign


def lane_sign(count):
    lane = lax.broadcasted_iota(jnp.int32, (count, 2 * SLOT), 1)
    return jnp.where(lane < SLOT, -1.0, 1.0).astype(jnp.float32)


def first_kernel(rows, table, out, held):
    sign = lane_sign(FIRST)

    def hold(spectrum, carry):
        for term in range(FIRST):
            held[spectrum, term * PITCH : term * PITCH + 16] = rows[spectrum, term].astype(
                jnp.float32
            )
        return carry

    lax.fori_loop(0, NSPEC, hold, 0)
    for place in range(16):
        columns = []
        for spectrum in range(NSPEC):
            picked = held[spectrum, pl.ds(place, FIRST, stride=PITCH), :]
            columns.append(
                jnp.concatenate([picked, quarter_turn(picked, sign)], axis=0).astype(jnp.bfloat16)
            )
        sums = jnp.dot(
            table[place],
            jnp.concatenate(columns, axis=1),
            preferred_element_type=jnp.float32,
        ).astype(jnp.bfloat16)
        for spectrum in range(NSPEC):
            out[spectrum, place] = sums[:, spectrum * 128 : spectrum * 128 + 128]


def second_kernel(rows, table, gains, out, held, scales):
    second_len = NCH // FIRST
    sign = lane_sign(second_len)
    low = sign < 0.0
    for place in range(16):
        gain = gains[place] * NCH ** (-0.5)
        other = pltpu.roll(gain, SLOT, 1)
        scales[0, place] = jnp.where(low, gain, other)
        scales[1, place] = jnp.where(low, -other, gain)

    def spectrum_step(spectrum, carry):
        for term in range(second_len):
            held[term * PITCH : term * PITCH + 16] = rows[spectrum, term].astype(jnp.float32)
        for pair in range(8):
            columns = []
            for place in (2 * pair, 2 * pair + 1):
                picked = held[pl.ds(place, second_len, stride=PITCH), :]
                columns.append(
                    jnp.concatenate([picked, quarter_turn(picked, sign)], axis=0).astype(
                        jnp.bfloat16
                    )
                )
            sums = jnp.dot(
                table[...],
                jnp.concatenate(columns, axis=1),
                preferred_element_type=jnp.float32,
            )
            for inner in range(2):
                place = 2 * pair + inner
                value = sums[:, inner * 128 : inner * 128 + 128]
                out[place, spectrum] = (
                    value * scales[0, place] + pltpu.roll(value, SLOT, 1) * scales[1, place]
                ).astype(jnp.bfloat16)
        return carry

    lax.fori_loop(0, NSPEC, spectrum_step, 0)


def spectra_of(voltages, gains):
    inputs_here = voltages.shape[1]
    second_len = NCH // FIRST
    frames = NSPEC + TAPS - 1
    chunk = 2 * second_len
    chunks = NCH // chunk
    lanes = 2 * SLOT
    first, second = combine_tables()
    params = pltpu.CompilerParams(
        dimension_semantics=("arbitrary",), vmem_limit_bytes=48 * 1024 * 1024
    )
    filtered = pl.pallas_call(
        filter_kernel,
        grid=(chunks,),
        in_specs=[
            pl.BlockSpec((2, inputs_here, chunk), lambda step, frame=frame: (0, 0, frame * chunks + step))
            for frame in range(frames)
        ]
        + [pl.BlockSpec((TAPS, chunk), lambda step: (0, step))],
        out_specs=pl.BlockSpec((NSPEC, 2, second_len, lanes), lambda step: (0, step, 0, 0)),
        out_shape=jax.ShapeDtypeStruct((NSPEC, FIRST, second_len, lanes), jnp.bfloat16),
        compiler_params=params,
        name="fir",
    )(*([voltages] * frames), coefficients())
    turned = pl.pallas_call(
        first_kernel,
        grid=(second_len // 16,),
        in_specs=[
            pl.BlockSpec((NSPEC, FIRST, 16, lanes), lambda step: (0, 0, step, 0)),
            pl.BlockSpec((16, FIRST, 2 * FIRST), lambda step: (step, 0, 0)),
        ],
        out_specs=pl.BlockSpec((NSPEC, 16, FIRST, lanes), lambda step: (0, step, 0, 0)),
        out_shape=jax.ShapeDtypeStruct((NSPEC, second_len, FIRST, lanes), jnp.bfloat16),
        scratch_shapes=[pltpu.VMEM((NSPEC, FIRST * PITCH, lanes), jnp.float32)],
        compiler_params=params,
        name="first_sums",
    )(filtered, first)
    arranged = jnp.transpose(
        gains.reshape(2, inputs_here, second_len, FIRST), (3, 2, 0, 1)
    )
    if inputs_here < SLOT:
        arranged = jnp.pad(arranged, ((0, 0), (0, 0), (0, 0), (0, SLOT - inputs_here)))
    return pl.pallas_call(
        second_kernel,
        grid=(FIRST // 16,),
        in_specs=[
            pl.BlockSpec((NSPEC, second_len, 16, lanes), lambda step: (0, 0, step, 0)),
            pl.BlockSpec((second_len, 2 * second_len), lambda step: (0, 0)),
            pl.BlockSpec((16, second_len, lanes), lambda step: (step, 0, 0)),
        ],
        out_specs=pl.BlockSpec((16, NSPEC, second_len, lanes), lambda step: (step, 0, 0, 0)),
        out_shape=jax.ShapeDtypeStruct((FIRST, NSPEC, second_len, lanes), jnp.bfloat16),
        scratch_shapes=[pltpu.VMEM((second_len * PITCH, lanes), jnp.float32),
            pltpu.VMEM((2, 16, second_len, lanes), jnp.float32),
        ],
        compiler_params=params,
        name="second_sums",
    )(turned, second, arranged.reshape(FIRST, second_len, lanes))


def phase_tables(offsets):
    turn = offsets * (2.0 * math.pi / NCH)
    both = jnp.concatenate([turn, turn], axis=1)
    eight = jnp.arange(8, dtype=jnp.float32)
    near = eight[:, None, None] * both[None]
    near_cos, near_sin = jnp.cos(near)[:, None], jnp.sin(near)[:, None]
    far = (FIRST * eight)[:, None, None] * both[None]
    far_cos, far_sin = jnp.cos(far)[None], jnp.sin(far)[None]
    fine = jnp.stack(
        [near_cos * far_cos - near_sin * far_sin, near_sin * far_cos + near_cos * far_sin]
    ).reshape(2, RUN, NBEAM, 2 * SLOT)
    middle = (8.0 * jnp.arange(FIRST // 8, dtype=jnp.float32))[:, None, None] * both[None]
    blocks = NCH // FIRST // 8
    wide = (8.0 * FIRST * jnp.arange(blocks, dtype=jnp.float32))[:, None, None] * turn[None]
    wide_cos = jnp.cos(wide)
    wide_sin = jnp.sin(wide)
    scale = NIN ** (-0.5)
    return (
        fine,
        jnp.stack([jnp.cos(middle), jnp.sin(middle)]),
        jnp.stack(
            [
                jnp.concatenate([wide_cos, wide_sin], axis=2) * scale,
                jnp.concatenate([wide_sin, -wide_cos], axis=2) * scale,
            ]
        ),
    )


def beam_kernel(step, spectra, fine, middle, wide, out):
    lanes = 2 * SLOT
    bases = []
    for half in range(2):
        coarse = 2 * (step // (FIRST // 8)) + half
        rest = step % (FIRST // 8)
        wide_cos = wide[0, coarse]
        wide_sin = wide[1, coarse]
        middle_cos = middle[0, rest]
        middle_sin = middle[1, rest]
        bases.append(
            (
                wide_cos * middle_cos - wide_sin * middle_sin,
                wide_sin * middle_cos + wide_cos * middle_sin,
            )
        )
    lane = lax.broadcasted_iota(jnp.int32, (NBEAM, 2 * lanes), 1)
    member = lane % 8
    sign = jnp.where(
        lax.broadcasted_iota(jnp.int32, (8 * NSPEC, lanes), 1) < SLOT, 1.0, -1.0
    ).astype(jnp.float32)
    blank = jnp.zeros((16 * NSPEC, lanes), jnp.bfloat16)

    def group(index):
        rights = []
        both = spectra[index].astype(jnp.float32)
        for half in range(2):
            block = both[:, half * 8 : half * 8 + 8].reshape(8 * NSPEC, lanes)
            swapped = pltpu.roll(block, SLOT, 1) * sign
            rights.append(jnp.concatenate([block, swapped], axis=0).astype(jnp.bfloat16))
        right = jnp.concatenate(
            [
                jnp.concatenate([rights[0], blank], axis=1),
                jnp.concatenate([blank, rights[1]], axis=1),
            ],
            axis=0,
        )
        lefts = []
        for inner in range(8):
            fine_cos = fine[0, index * 8 + inner]
            fine_sin = fine[1, index * 8 + inner]
            lefts.append(
                jnp.concatenate(
                    [
                        (base_cos * fine_cos - base_sin * fine_sin).astype(jnp.bfloat16)
                        for base_cos, base_sin in bases
                    ],
                    axis=1,
                )
            )
        products = lax.dot_general(
            jnp.concatenate(lefts, axis=0),
            right,
            (((1,), (1,)), ((), ())),
            preferred_element_type=jnp.float32,
        )
        total = products[:NBEAM]
        for inner in range(1, 8):
            total = jnp.where(
                member == inner, products[inner * NBEAM : (inner + 1) * NBEAM], total
            )
        return total

    def pair(index, carry):
        low = group(2 * index)
        high = group(2 * index + 1)
        for unit in range(8):
            rows = slice(unit * 8, unit * 8 + 8)
            both = jnp.concatenate([low[rows], high[rows]], axis=0).astype(jnp.bfloat16)
            out[unit % 2, 0, unit // 2, pl.ds(index * 16, 16), :] = both
        return carry

    lax.fori_loop(0, RUN // 16, pair, 0, unroll=4)


def partial_beams(spectra, tables, across, chunk, chunks):
    share = NCH // (2 * RUN) // across // chunks
    runs = share * across
    fine, middle, wide = tables
    whole = lambda array: pl.BlockSpec(array.shape, lambda step: (0,) * array.ndim)

    def run_of(step):
        return step // share * (share * chunks) + chunk * share + step % share

    def kernel(spectra, fine, middle, wide, out):
        beam_kernel(run_of(pl.program_id(0)), spectra, fine, middle, wide, out)

    return pl.pallas_call(
        kernel,
        grid=(runs,),
        in_specs=[
            pl.BlockSpec(
                (8, NSPEC, 16, 2 * SLOT),
                lambda step: (run_of(step) % (FIRST // 8), 0, run_of(step) // (FIRST // 8), 0),
            ),
            whole(fine),
            whole(middle),
            whole(wide),
        ],
        out_specs=pl.BlockSpec((2, 1, 4, RUN, 4 * SLOT), lambda step: (0, step, 0, 0, 0)),
        out_shape=jax.ShapeDtypeStruct((2, runs, 4, RUN, 4 * SLOT), jnp.bfloat16),
        compiler_params=pltpu.CompilerParams(
            dimension_semantics=("arbitrary",), vmem_limit_bytes=48 * 1024 * 1024
        ),
        cost_estimate=pl.CostEstimate(
            flops=2 * runs * RUN * NBEAM * 256 * 256,
            bytes_accessed=runs * RUN * (2 * 8 + 4 * 8) * 2 * SLOT * 2,
            transcendentals=0,
        ),
        name="beam_sums",
    )(spectra, fine, middle, wide)


def detect(beams):
    runs, groups, count, lanes = beams.shape
    wide = beams.astype(jnp.bfloat16).astype(jnp.float32)
    source = jnp.arange(lanes, dtype=jnp.int32)
    source_half = source // (16 * NSPEC)
    source_channel = source % 8
    source_time = source // 8 % NSPEC // INTEG
    place = (source_half * TIMES + source_time) * 8 + source_channel
    pick = (place[:, None] == jnp.arange(2 * TIMES * 8, dtype=jnp.int32)[None]).astype(jnp.float32)
    power = jnp.einsum(
        "tgrl,lm->tgrm",
        wide * wide,
        pick,
        precision=lax.Precision.HIGHEST,
        preferred_element_type=jnp.float32,
    )
    parts = FIRST // 8
    power = power.reshape(runs // parts, parts, groups, count, 2, TIMES, 8)
    return jnp.transpose(power, (3, 5, 0, 4, 6, 1, 2)).reshape(count, TIMES, runs * 2 * groups * 8)


def body(voltages, gains, delays, channel_order, beam_table):
    across = lax.axis_size("gx")
    along = lax.axis_size("gy")
    inputs_here = voltages.shape[1]
    beams_here = NBEAM // along
    column = lax.axis_index("gx")
    member = lax.axis_index("gy")
    first_input = (column * along + member) * inputs_here
    offsets = jnp.take(
        lax.dynamic_slice_in_dim(delays, first_input, inputs_here, 1), beam_table, axis=0
    )
    if inputs_here < SLOT:
        offsets = jnp.pad(offsets, ((0, 0), (0, SLOT - inputs_here)))
    spectra = spectra_of(voltages, gains)
    tables = phase_tables(offsets)
    groups = RUN // 8
    lanes = 4 * SLOT
    pairs = [[2 * index, 2 * index + 1] for index in range(along // 2)]
    evens = [[2 * index + odd for index in range(along // 2)] for odd in range(2)]
    chunks = CHUNKS

    def exchange(share):
        return lax.all_to_all(share, "gy", 0, 0, tiled=True, axis_index_groups=evens)

    shares = []
    pieces = []
    for chunk in range(chunks):
        held_back = [shares[chunk - 2]] if chunk >= 2 else []
        held_back += [pieces[chunk - 3]] if chunk >= 3 else []
        tables, held_back = lax.optimization_barrier((tables, held_back))
        if chunk >= 2:
            shares[chunk - 2] = held_back[0]
            pieces.append(exchange(shares[chunk - 2]))
        if chunk >= 3:
            pieces[chunk - 3] = held_back[1]
        partial = partial_beams(spectra, tables, across, chunk, chunks)
        runs = partial.shape[1]
        if beams_here != 8:
            partial = jnp.transpose(
                partial.reshape(2, runs, 4, groups, 8, lanes), (2, 0, 4, 1, 3, 5)
            ).reshape(along // 2, 2, beams_here, runs, groups, lanes)
            partial = jnp.transpose(partial, (1, 3, 0, 4, 2, 5)).reshape(
                2, runs, along // 2, groups * beams_here, lanes
            )
        halves = lax.all_to_all(partial, "gy", 0, 0, tiled=True, axis_index_groups=pairs)
        chip = (halves[0].astype(jnp.float32) + halves[1].astype(jnp.float32)).astype(jnp.bfloat16)
        column_sum = lax.psum_scatter(chip, "gx", scatter_dimension=0, tiled=True)
        shares.append(jnp.transpose(column_sum, (1, 0, 2, 3)))
    pieces += [exchange(share) for share in shares[len(pieces) :]]
    beams = jnp.concatenate([piece.astype(jnp.float32).sum(axis=0) for piece in pieces], axis=0)
    power = detect(beams.reshape(-1, groups, beams_here, lanes))
    width = NCH // (across * along)
    order = channel_order[column]
    return jnp.take(power.reshape(beams_here, TIMES, along, width), order, axis=2).reshape(
        beams_here, TIMES, along * width
    )


def solution(mesh):
    return jax.shard_map(
        body,
        mesh=mesh,
        in_specs=(P(None, ("gx", "gy"), None), P(None, ("gx", "gy"), None), P(), P(), P()),
        out_specs=P("gy", None, "gx"),
        check_vma=False,
    )
```

time: 806 us -> 355 us (0.44)
  local copies, waits for them, and re-layouts: 280 us -> 35.9 us
  other arithmetic: 152 us -> 23.8 us
  waiting for transfers between devices: 177 us -> 78.5 us
  Pallas kernels: 110 us -> 160 us
  matrix products: 39.8 us -> 3.49 us
  starting transfers between devices: 0.04 us -> 9.21 us
    transpose x2 -> x0, other arithmetic: 95.7 us -> none  [the longest x1 85.1 us: transform(): jnp.transpose(filtered.reshape(2, inputs_here, spectra_here, first_len, s...]
    another operation x2 -> x0, local copies, waits for them, and re-layouts: 93.7 us -> none  [partial_beams(): spectra.reshape(NCH // RUN, RUN, NSPEC, 2 * SLOT)]
    unnamed x3 -> x2, waiting for transfers between devices: 87.8 us -> 0.03 us
    reshape x3 -> x2, local copies, waits for them, and re-layouts: 92.1 us -> 16.8 us  [the longest x1 8.9 us: spectra_of(): arranged.reshape(FIRST, second_len, lanes)]
    slice x4 -> x0, local copies, waits for them, and re-layouts: 67.5 us -> none  [the longest x2 44.6 us: transform(): outer[:, :, second_len:].reshape(inputs_here, spectra_here, NCH) * scale]
    pallas_call x1 -> x5, Pallas kernels: 110 us -> 160 us  [the longest x2 66.9 us: partial_beams(): pl.pallas_call(kernel, grid=(runs,), in_specs=[pl.BlockSpec((8, NSPEC, 16...]
    dot_general x2 -> x0, matrix products: 36.3 us -> none  [the longest x1 21.4 us: transform(): jnp.einsum('km,ismq->iskq', small_stack, stacked, preferred_element_type=...]
    reduce_scatter x1 -> x2, waiting for transfers between devices: 89.1 us -> 53.3 us  [body(): column_sum = lax.psum_scatter(chip, 'gx', scatter_dimension=0, tiled=True)]
  transfers between devices with their start and end apart: 2 -> 4, of which waited for: 2 -> 3; matrix products, arithmetic and copies ran while one was open for 0% -> 2% of each run, Pallas kernels for 0% -> 10%
where the time goes in v2:
time: 355 us; the launch traced here: 350 us
  Pallas kernels  160 us (45%)
  waiting for transfers between devices  78.5 us (22%)
  local copies, waits for them, and re-layouts  35.9 us (10%)
  blocking collectives  24.2 us (7%)
  other arithmetic  23.8 us (7%)
  between operations  14.4 us (4%)
  starting transfers between devices  9.21 us (3%)
    pallas_call x2, Pallas kernels, partial_beams(): pl.pallas_call(kernel, grid=(runs,), in_specs=[pl.BlockSpec((8, NSPEC, 16...  66.9 us
    reduce_scatter x2, waiting for transfers between devices, body(): column_sum = lax.psum_scatter(chip, 'gx', scatter_dimension=0, tiled=True)  53.3 us
    pallas_call x1, Pallas kernels, spectra_of(): pl.pallas_call(second_kernel, grid=(FIRST // 16,), in_specs=[pl.BlockSpec...  37.2 us
    pallas_call x1, Pallas kernels, spectra_of(): pl.pallas_call(filter_kernel, grid=(chunks,), in_specs=[pl.BlockSpec((2,...  36.1 us
    all_to_all x2, waiting for transfers between devices, exchange(): lax.all_to_all(share, 'gy', 0, 0, tiled=True, axis_index_groups=evens)  25.2 us
    all_to_all x2, blocking collectives, body(): lax.all_to_all(partial, 'gy', 0, 0, tiled=True, axis_index_groups=pairs)  24.2 us
    pallas_call x1, Pallas kernels, spectra_of(): pl.pallas_call(first_kernel, grid=(second_len // 16,), in_specs=[pl.Block...  20 us
    all_to_all x2, starting transfers between devices, exchange(): lax.all_to_all(share, 'gy', 0, 0, tiled=True, axis_index_groups=evens)  9.16 us
  transfers between devices with their start and end apart: 4, of which 3 were waited for; matrix products, arithmetic and copies ran while one was open for 2% of the time, Pallas kernels for 10%

profile of v2, /device:TPU:0, one launch (start us, length us, event | category | flops | bytes accessed | tf_op | source)
XLA Modules:
  0.0 349.6 jit_solution(14107394432354844147)
XLA Ops:
  14.3 7.9 %reshape.387 = f32[2,64,128,64]{3,2,1,0:T(8,128)} reshape(f32[2,64,8192]{2,1,0:T(8,128)} %param.6) | data formatting | bytes 8388608 | tf_op jit(solution)/shard_map/reshape | solution.py:193
  22.2 8.9 %copy.18.gains = f32[64,128,128]{2,1,0:T(8,128)} copy(f32[64,128,128]{0,1,2:T(8,128)} %bitcast.41) | data formatting | bytes 8388608 | tf_op jit(solution)/shard_map/reshape | solution.py:212
  34.8 1.9 fusion.3
  38.4 36.1 %fir.1.rows = bf16[8,64,128,128]{3,2,1,0:T(8,128)(2,1)} custom-call(bf16[2,64,122880]{2,1,0:T(8,128)(2,1)} %refs_14_.1, bf16[2,64,122880]{2,1,0:T(8,128)(2,1)} %refs_14_.1, bf16[2,64,122880]{2,1,0:T(8,128)(2,1)} %refs_14_.1, bf16[2,64,122880]{2,1,0:T(8,128)(2,1)} %refs_14_.1, bf16[2,64,122880]{2,1,0:T(8,128)(2,1)} %refs_14_.1, ...), custom_call_target="tpu_custom_call" | custom-call | tf_op jit(solution)/shard_map/fir/pallas_call | solution.py:166
  74.5 2.5 subtract_convert_fusion
  78.2 20.0 %first_sums.1.rows = bf16[8,128,64,128]{3,2,1,0:T(8,128)(2,1)} custom-call(bf16[8,64,128,128]{3,2,1,0:T(8,128)(2,1)} %fir.1.rows, bf16[128,64,128]{2,1,0:T(8,128)(2,1)S(1)} %pad_maximum_fusion.1.table), custom_call_target="tpu_custom_call" | custom-call | tf_op jit(solution)/shard_map/first_sums/pallas_call | solution.py:179
  98.2 37.2 %second_sums.1.spectra = bf16[64,8,128,128]{3,2,1,0:T(8,128)(2,1)} custom-call(bf16[8,128,64,128]{3,2,1,0:T(8,128)(2,1)} %first_sums.1.rows, bf16[128,256]{1,0:T(8,128)(2,1)S(1)} %pad_maximum_fusion.4.table, f32[64,128,128]{2,1,0:T(8,128)S(1)} %copy-done.2), custom_call_target="tpu_custom_call" | custom-call | tf_op jit(solution)/shard_map/second_sums/pallas_call | solution.py:197
  135.5 33.4 %beam_sums.3 = bf16[2,32,4,64,256]{4,3,2,1,0:T(8,128)(2,1)} custom-call(bf16[64,8,128,128]{3,2,1,0:T(8,128)(2,1)} %second_sums.1.spectra, f32[2,64,64,128]{3,2,1,0:T(8,128)S(1)} %pad_maximum_fusion.fine, f32[2,8,64,128]{3,2,1,0:T(8,128)S(1)} %pad_maximum_fusion.3.middle, f32[2,16,64,128]{3,2,1,0:T(8,128)S(1)} %pad_maximum_fusion.2.wide), custom_call_target="tpu_custom_call" | custom-call | flops 17179869184 | bytes 25165824 | tf_op jit(solution)/shard_map/beam_sums/pallas_call | solution.py:331
  168.8 12.1 %all_to_all.20 = bf16[2,32,4,64,256]{4,3,2,1,0:T(8,128)(2,1)S(1)} all-to-all(bf16[2,32,4,64,256]{4,3,2,1,0:T(8,128)(2,1)} %beam_sums.3), channel_id=1, replica_groups={{0,1},{2,3},{4,5},{6,7},{8,9},{10,11},{12,13},{14,15},{16,17},{18,19},{..., dimensions={0} | all-to-all | bytes 16777216 | tf_op jit(solution)/shard_map/all_to_all | solution.py:422
  180.9 3.0 fusion.1
  184.0 2.2 copy-done.4
  186.2 33.6 %beam_sums.2 = bf16[2,32,4,64,256]{4,3,2,1,0:T(8,128)(2,1)} custom-call(bf16[64,8,128,128]{3,2,1,0:T(8,128)(2,1)} %second_sums.1.spectra, f32[2,64,64,128]{3,2,1,0:T(8,128)S(1)} %copy-done.4, f32[2,8,64,128]{3,2,1,0:T(8,128)S(1)} %pad_maximum_fusion.3.middle, f32[2,16,64,128]{3,2,1,0:T(8,128)S(1)} %pad_maximum_fusion.2.wide), custom_call_target="tpu_custom_call" | custom-call | flops 17179869184 | bytes 25165824 | tf_op jit(solution)/shard_map/beam_sums/pallas_call | solution.py:331
  219.7 12.1 %all_to_all.21 = bf16[2,32,4,64,256]{4,3,2,1,0:T(8,128)(2,1)S(1)} all-to-all(bf16[2,32,4,64,256]{4,3,2,1,0:T(8,128)(2,1)} %beam_sums.2), channel_id=1, replica_groups={{0,1},{2,3},{4,5},{6,7},{8,9},{10,11},{12,13},{14,15},{16,17},{18,19},{..., dimensions={0} | all-to-all | bytes 16777216 | tf_op jit(solution)/shard_map/all_to_all | solution.py:422
  231.8 3.0 fusion
  234.8 4.6 %reduce-scatter.5.cloned.1.call-done = bf16[8,4,64,256]{3,2,1,0:T(8,128)(2,1)} async-done(((bf16[32,4,64,256]{3,2,1,0:T(8,128)(2,1)}), bf16[8,4,64,256]{3,2,1,0:T(8,128)(2,1)}) %reduce-scatter.5.cloned.1.call-update) | async-done | bytes 1048592 | tf_op jit(solution)/shard_map/reduce_scatter | solution.py:424
  239.4 2.4 copy.20
  241.8 4.6 %all-to-all-start.3 = ((bf16[4,8,64,256]{3,2,1,0:T(8,128)(2,1)}), bf16[4,8,64,256]{3,2,1,0:T(8,128)(2,1)S(1)}, u32[]{:S(2)}, u32[]{:S(2)}) async-start(bf16[4,8,64,256]{3,2,1,0:T(8,128)(2,1)} %copy.20), calls=%async_computation.5 | async-start | bytes 2097152 | tf_op jit(solution)/shard_map/all_to_all | solution.py:400
  246.4 48.7 %reduce-scatter.3.cloned.1.call-done = bf16[8,4,64,256]{3,2,1,0:T(8,128)(2,1)} async-done(((bf16[32,4,64,256]{3,2,1,0:T(8,128)(2,1)}), bf16[8,4,64,256]{3,2,1,0:T(8,128)(2,1)}) %reduce-scatter.3.cloned.1.call-update) | async-done | bytes 1048592 | tf_op jit(solution)/shard_map/reduce_scatter | solution.py:424
  295.1 2.3 copy.19
  297.4 4.6 %all-to-all-start.1 = ((bf16[4,8,64,256]{3,2,1,0:T(8,128)(2,1)}), bf16[4,8,64,256]{3,2,1,0:T(8,128)(2,1)S(1)}, u32[]{:S(2)}, u32[]{:S(2)}) async-start(bf16[4,8,64,256]{3,2,1,0:T(8,128)(2,1)} %copy.19), calls=%async_computation.2 | async-start | bytes 2097152 | tf_op jit(solution)/shard_map/all_to_all | solution.py:400
  302.3 25.2 %all-to-all-done.1 = bf16[4,8,64,256]{3,2,1,0:T(8,128)(2,1)S(1)} async-done(((bf16[4,8,64,256]{3,2,1,0:T(8,128)(2,1)}), bf16[4,8,64,256]{3,2,1,0:T(8,128)(2,1)S(1)}, u32[]{:S(2)}, u32[]{:S(2)}) %all-to-all-start.1) | async-done | bytes 1048608 | tf_op jit(solution)/shard_map/all_to_all | solution.py:400
  327.8 3.5 convolution_bitcast_fusion
  331.3 5.8 %copy.21 = f32[8,4,2,2,8,8,8]{6,5,4,3,2,1,0:T(8,128)} copy(f32[8,4,2,2,8,8,8]{4,0,1,3,6,5,2:T(8,128)} %convolution_bitcast_fusion) | data formatting | bytes 524288 | tf_op jit(solution)/shard_map/transpose | solution.py:375
  337.1 4.0 %reshape_reshape.3 = f32[8,4,8,256]{3,2,1,0:T(8,128)S(1)} reshape(f32[8,4,2,2,8,8,8]{6,5,4,3,2,1,0:T(8,128)} %copy.21) | data formatting | bytes 524288 | tf_op jit(solution)/shard_map/reshape;reshape | solution.py:431
  (67 shorter events, 16.0 us)
Async XLA Ops:
  6.5 24.6 %copy-start = (f32[64,2048]{1,0:T(8,128)S(1)}, f32[64,2048]{1,0:T(8,128)}, u32[]{:S(2)}) copy-start(f32[64,2048]{1,0:T(8,128)} %param.7) | copy-start | bytes 1572868
  6.5 232.9 %reduce-scatter.5.cloned.1.call-start = ((), (), s32[]{:S(2)}) async-start(), calls=%async_computation.7 | async-start | bytes 5242880 | tf_op jit(solution)/shard_map/reduce_scatter | solution.py:424
  37.9 97.6 %copy-start.3 = (f32[2,64,64,128]{3,2,1,0:T(8,128)}, f32[2,64,64,128]{3,2,1,0:T(8,128)S(1)}, u32[]{:S(2)}) copy-start(f32[2,64,64,128]{3,2,1,0:T(8,128)S(1)} %pad_maximum_fusion.fine) | copy-start | bytes 12582916
  38.4 36.1 %copy-start.5 = (f32[128,64]{1,0:T(8,128)S(1)}, f32[128,64]{1,0:T(8,128)}, u32[]{:S(2)}) copy-start(f32[128,64]{1,0:T(8,128)} %get-tuple-element.32) | copy-start | bytes 98308
  38.4 36.1 %copy-start.6 = (f32[128,64]{1,0:T(8,128)S(1)}, f32[128,64]{1,0:T(8,128)}, u32[]{:S(2)}) copy-start(f32[128,64]{1,0:T(8,128)} %get-tuple-element.33) | copy-start | bytes 98308
  38.4 36.1 %copy-start.7 = (f32[64,64]{1,0:T(8,128)S(1)}, f32[64,64]{1,0:T(8,128)}, u32[]{:S(2)}) copy-start(f32[64,64]{1,0:T(8,128)} %get-tuple-element.34) | copy-start | bytes 49156
  38.4 36.1 %copy-start.8 = (f32[64,64]{1,0:T(8,128)S(1)}, f32[64,64]{1,0:T(8,128)}, u32[]{:S(2)}) copy-start(f32[64,64]{1,0:T(8,128)} %get-tuple-element.35) | copy-start | bytes 49156
  78.2 20.0 %copy-start.9 = (bf16[128,128]{1,0:T(8,128)(2,1)S(1)}, bf16[128,128]{1,0:T(8,128)(2,1)}, u32[]{:S(2)}) copy-start(bf16[128,128]{1,0:T(8,128)(2,1)} %get-tuple-element.36) | copy-start | bytes 98308
  78.2 20.0 %copy-start.10 = (bf16[128,128]{1,0:T(8,128)(2,1)S(1)}, bf16[128,128]{1,0:T(8,128)(2,1)}, u32[]{:S(2)}) copy-start(bf16[128,128]{1,0:T(8,128)(2,1)} %get-tuple-element.37) | copy-start | bytes 98308
  78.2 20.0 %copy-start.2 = (f32[64,128,128]{2,1,0:T(8,128)S(1)}, f32[64,128,128]{2,1,0:T(8,128)}, u32[]{:S(2)}) copy-start(f32[64,128,128]{2,1,0:T(8,128)} %copy.18.gains) | copy-start | bytes 12582916
  183.9 111.1 %reduce-scatter.3.cloned.1.call-start = ((), (), s32[]{:S(2)}) async-start(), calls=%async_computation.6 | async-start | bytes 5242880 | tf_op jit(solution)/shard_map/reduce_scatter | solution.py:424
  184.0 2.2 copy-start.4
  239.4 62.5 %copy-start.11 = (s32[4,8]{1,0:T(4,128)S(1)}, s32[4,8]{1,0:T(4,128)}, u32[]{:S(2)}) copy-start(s32[4,8]{1,0:T(4,128)} %param.8) | copy-start | bytes 388
  241.8 55.6 %all-to-all-start.3 = ((bf16[4,8,64,256]{3,2,1,0:T(8,128)(2,1)}), bf16[4,8,64,256]{3,2,1,0:T(8,128)(2,1)S(1)}, u32[]{:S(2)}, u32[]{:S(2)}) async-start(bf16[4,8,64,256]{3,2,1,0:T(8,128)(2,1)} %copy.20), calls=%async_computation.5 | async-start | bytes 2097152 | tf_op jit(solution)/shard_map/all_to_all | solution.py:400
  297.4 30.1 %all-to-all-start.1 = ((bf16[4,8,64,256]{3,2,1,0:T(8,128)(2,1)}), bf16[4,8,64,256]{3,2,1,0:T(8,128)(2,1)S(1)}, u32[]{:S(2)}, u32[]{:S(2)}) async-start(bf16[4,8,64,256]{3,2,1,0:T(8,128)(2,1)} %copy.19), calls=%async_computation.2 | async-start | bytes 2097152 | tf_op jit(solution)/shard_map/all_to_all | solution.py:400
  331.3 11.5 %copy-start.1 = (f32[64,2048]{1,0:T(8,128)S(1)}, f32[64,2048]{1,0:T(8,128)}, u32[]{:S(2)}) copy-start(f32[64,2048]{1,0:T(8,128)} %param.7) | copy-start | bytes 1572868
Sparse Core Ops, SparseCore 0:
  184.1 55.3 reduce-scatter.4
  242.4 52.5 reduce-scatter.2
